TPU v7x, 32 devices: a 4x4x1 block of a 4x4x8 slice. The times are simulated.
32 devices in a mesh: member: 1 (over z), lon: 4 (over y), lat: 8 (over x, core).
Axes of the slice: x: 4, y: 4, z: 1, core: 2. Of those that a mesh axis runs over, the one named last changes fastest.
The devices are a block of a 4x4x8 slice.
Arguments:
- field_in: float32 [4, 256, 256, 512], P('member', None, 'lat', 'lon')
- fwd_table: float32 [256, 256, 256], replicated
- inv_table: float32 [256, 256, 256], replicated
- mix_weights: float32 [256, 256, 256, 2], replicated
Outputs:
- output: float32 [4, 256, 256, 512], P('member', None, 'lat', 'lon')
All inputs are finite; a program needn't handle non-finite values.
Results may differ from a plain program's by a relative error of at most 0.00315129.
Values are sent between devices in bfloat16 or wider.
A program may use at most 768 MiB of HBM per device.

v0:
```python
import math
import jax
import jax.numpy as jnp
from jax import lax
from jax.sharding import PartitionSpec as P


def dft_tables(lon_points, wave_ids):
    lon_ids = jnp.arange(lon_points)
    phase_arg = (2.0 * math.pi / lon_points) * ((lon_ids[:, None] * wave_ids[None, :]) % lon_points).astype(jnp.float32)
    cos_val = jnp.cos(phase_arg)
    sin_val = jnp.sin(phase_arg)
    weight_m = jnp.where(wave_ids == 0, 1.0, 2.0).astype(jnp.float32)
    fwd_dft = jnp.stack([cos_val, -sin_val], axis=1).astype(jnp.bfloat16)
    inv_dft = jnp.stack([(weight_m * cos_val).T, (-weight_m * sin_val).T], axis=0).astype(jnp.bfloat16)
    return fwd_dft, inv_dft


def solution(mesh):
    lon_count = mesh.shape['lon']
    grid_spec = P('member', None, 'lat', 'lon')

    def local_layer(field_in, fwd_table, inv_table, mix_weights):
        lon_points = field_in.shape[3] * lon_count
        degrees = fwd_table.shape[1]
        fwd_dft, inv_dft = dft_tables(lon_points, jnp.arange(degrees))
        grid_bf = field_in.astype(jnp.bfloat16)
        lon_full = lax.all_to_all(grid_bf, 'lon', 1, 3, tiled=True)
        spec_all = jnp.einsum('sctj,jrm->sctrm', lon_full, fwd_dft, preferred_element_type=jnp.float32).astype(jnp.bfloat16)
        spec_loc = lax.all_to_all(spec_all, 'lat', 4, 2, tiled=True)
        coef_loc = jnp.einsum('mlt,sctrm->sclrm', fwd_table.astype(jnp.bfloat16), spec_loc, preferred_element_type=jnp.float32).astype(jnp.bfloat16)
        coef_chan = lax.all_to_all(coef_loc, 'lon', 2, 1, tiled=True)
        w_bf = mix_weights.astype(jnp.bfloat16)
        w_re = w_bf[..., 0]
        w_im = w_bf[..., 1]
        w_block = jnp.stack([jnp.stack([w_re, -w_im], axis=-1), jnp.stack([w_im, w_re], axis=-1)], axis=2)
        mixed_chan = jnp.einsum('loqir,silrm->solqm', w_block, coef_chan, preferred_element_type=jnp.float32).astype(jnp.bfloat16)
        mixed_loc = lax.all_to_all(mixed_chan, 'lon', 1, 2, tiled=True)
        back_loc = jnp.einsum('mlt,sclrm->sctrm', inv_table.astype(jnp.bfloat16), mixed_loc, preferred_element_type=jnp.float32).astype(jnp.bfloat16)
        back_all = lax.all_to_all(back_loc, 'lat', 2, 4, tiled=True)
        wave_loc = jnp.einsum('sctrm,rmj->sctj', back_all, inv_dft, preferred_element_type=jnp.float32).astype(jnp.bfloat16)
        wave_grid = lax.all_to_all(wave_loc, 'lon', 3, 1, tiled=True)
        return field_in + jax.nn.gelu(wave_grid.astype(jnp.float32), approximate=True)

    return jax.shard_map(local_layer, mesh=mesh, in_specs=(grid_spec, P('lat', None, None), P('lat', None, None), P('lon', None, None, None)), out_specs=grid_spec, check_vma=False)
```

profile of v0, /device:TPU:97, one launch (start us, length us, event | category | flops | bytes accessed | tf_op | source)
XLA Modules:
  0.0 1241.6 jit_solution(9386092686964258693)
XLA Ops:
  18.2 92.3 %all-to-all-done = bf16[4,256,32,128]{3,2,0,1:T(8,128)(2,1)} async-done(((bf16[4,256,32,128]{3,2,0,1:T(8,128)(2,1)}), bf16[4,256,32,128]{3,2,0,1:T(8,128)(2,1)}, u32[]{:S(2)}, u32[]{:S(2)}) %all-to-all-start) | async-done | bytes 8388640 | tf_op jit(solution)/shard_map/all_to_all | solution.py:28
  146.0 23.9 %copy.45 = bf16[4,64,32,2,256]{1,2,0,3,4:T(8,128)(2,1)} copy(bf16[4,64,32,2,256]{4,1,2,0,3:T(8,128)(2,1)} %convert_bitcast_fusion.3) | data formatting | bytes 16777216 | tf_op jit(solution)/shard_map/convert_element_type | solution.py:29
  194.6 92.2 %all-to-all-done.1 = bf16[8,2,262144]{2,1,0:T(2,128)(2,1)} async-done(((bf16[8,2,262144]{2,1,0:T(2,128)(2,1)}), bf16[8,2,262144]{2,1,0:T(2,128)(2,1)}, u32[]{:S(2)}, u32[]{:S(2)}) %all-to-all-start.1) | async-done | bytes 8388640 | tf_op jit(solution)/shard_map/all_to_all | solution.py:30
  303.3 18.7 %copy.47 = bf16[4,64,8,32,2,32]{1,5,4,3,2,0:T(8,128)(2,1)} copy(bf16[4,64,8,32,2,32]{1,3,0,4,5,2:T(8,128)(2,1)} %bitcast.109) | data formatting | bytes 16777216 | tf_op jit(solution)/shard_map/all_to_all | solution.py:30
  322.0 22.7 %convert_bitcast_fusion.2 = bf16[4,64,256,2,32]{2,1,3,0,4:T(8,128)(2,1)} fusion(bf16[4,64,256,2,32]{1,4,3,2,0:T(8,128)(2,1)} %bitcast.118, f32[256,256,256]{2,1,0:T(8,128)} %param.5, s32[]{:T(128)} %bitcast.9), kind=kOutput, calls=%fused_computation.27 | convolution fusion | flops 2151677952 | bytes 29360640 | tf_op jit(solution)/shard_map/mlt,sctrm->sclrm/dot_general | solution.py:31
  344.8 36.1 %copy.49 = bf16[4,64,256,2,32]{1,3,0,4,2:T(2,128)(2,1)} copy(bf16[4,64,256,2,32]{2,1,3,0,4:T(8,128)(2,1)} %convert_bitcast_fusion.2) | data formatting | bytes 16777216 | tf_op jit(solution)/shard_map/convert_element_type | solution.py:31
  380.8 17.0 %reshape.228 = bf16[4,2,524288]{2,1,0:T(2,128)(2,1)} reshape(bf16[256,32,4,2,64]{4,3,2,1,0:T(2,128)(2,1)} %bitcast.105) | data formatting | bytes 16777216
  438.1 21.4 %maximum_bitcast_fusion.2 = (bf16[64,256,1,256,2]{3,1,4,2,0:T(8,128)(2,1)}, bf16[64,256,1,256,2]{3,1,4,2,0:T(8,128)(2,1)}) fusion(bf16[64,256,256,1]{2,1,3,0:T(8,128)(2,1)S(1)} %get-tuple-element.5, bf16[64,256,256,1]{2,1,3,0:T(8,128)(2,1)} %get-tuple-element.7, bf16[64,256,256,1]{2,1,3,0:T(8,128)(2,1)} %get-tuple-element.6), kind=kLoop, calls=%fused_computation.15 | loop fusion | flops 16777216 | bytes 58720256 | tf_op jit(solution)/shard_map/stack | solution.py:36
  459.5 36.5 %all-to-all-done.2 = bf16[4,2,524288]{2,1,0:T(2,128)(2,1)} async-done(((bf16[4,2,524288]{2,1,0:T(2,128)(2,1)}), bf16[4,2,524288]{2,1,0:T(2,128)(2,1)}, u32[]{:S(2)}, u32[]{:S(2)}) %all-to-all-start.2) | async-done | bytes 8388640 | tf_op jit(solution)/shard_map/all_to_all | solution.py:32
  512.0 20.0 %copy.83 = bf16[4,64,4,64,2,32]{1,2,5,4,0,3:T(4,128)(2,1)} copy(bf16[4,64,4,64,2,32]{1,4,0,5,3,2:T(2,128)(2,1)} %bitcast.110) | data formatting | bytes 16777216 | tf_op jit(solution)/shard_map/all_to_all | solution.py:32
  532.0 24.2 %reshape.218 = bf16[4,256,64,2,32,1]{1,4,3,0,2,5:T(8,128)(2,1)} reshape(bf16[4,4,64,64,2,32]{2,1,5,4,0,3:T(4,128)(2,1)} %bitcast.111) | data formatting | bytes 16777216 | tf_op jit(solution)/shard_map/all_to_all | solution.py:32
  556.2 20.8 %fusion.16 = bf16[4,256,64,2,32]{1,4,3,0,2:T(8,128)(2,1)} fusion(bf16[64,256,1,256,2]{3,1,4,2,0:T(8,128)(2,1)} %get-tuple-element.9, bf16[64,256,1,256,2]{3,1,4,2,0:T(8,128)(2,1)} %get-tuple-element.8, bf16[4,256,64,2,32,1]{1,4,3,0,2,5:T(8,128)(2,1)} %reshape.218), kind=kOutput, calls=%fused_computation.31 | convolution fusion | flops 4366270464 | bytes 50331648 | tf_op jit(solution)/shard_map/loqir,silrm->solqm/dot_general | solution.py:37
  577.0 29.2 %copy.53 = bf16[4,256,64,2,32]{2,4,3,0,1:T(8,128)(2,1)} copy(bf16[4,256,64,2,32]{1,4,3,0,2:T(8,128)(2,1)} %fusion.16) | data formatting | bytes 16777216 | tf_op jit(solution)/shard_map/convert_element_type | solution.py:37
  622.9 98.6 %all_to_all.99 = bf16[4,2,524288]{2,1,0:T(2,128)(2,1)} all-to-all(bf16[4,2,524288]{2,1,0:T(2,128)(2,1)} %reshape.230), channel_id=1, replica_groups=mesh['member'=1,'lon'=4,'lat'=8] {'lon'}, dimensions={0} | all-to-all | bytes 16777216 | tf_op jit(solution)/shard_map/all_to_all | solution.py:38
  737.6 22.3 %copy.82 = bf16[4,4,64,64,2,32]{3,1,2,4,0,5:T(4,128)(2,1)} copy(bf16[4,4,64,64,2,32]{3,5,4,0,2,1:T(8,128)(2,1)} %bitcast.112) | data formatting | bytes 16777216 | tf_op jit(solution)/shard_map/all_to_all | solution.py:38
  759.8 24.2 %all_to_all.87 = bf16[4,64,256,2,32]{2,1,3,0,4:T(8,128)(2,1)} reshape(bf16[4,64,4,64,2,32]{3,2,1,4,0,5:T(4,128)(2,1)} %bitcast.113) | data formatting | bytes 16777216 | tf_op jit(solution)/shard_map/all_to_all | solution.py:38
  795.4 36.1 %copy.55 = bf16[4,64,256,2,32]{1,3,0,4,2:T(2,128)(2,1)} copy(bf16[4,64,256,2,32]{2,1,3,0,4:T(8,128)(2,1)} %convert_bitcast_fusion.1) | data formatting | bytes 16777216 | tf_op jit(solution)/shard_map/convert_element_type | solution.py:39
  860.8 89.4 %all-to-all-done.4 = bf16[8,2,262144]{2,1,0:T(2,128)(2,1)} async-done(((bf16[8,2,262144]{2,1,0:T(2,128)(2,1)}), bf16[8,2,262144]{2,1,0:T(2,128)(2,1)}, u32[]{:S(2)}, u32[]{:S(2)}) %all-to-all-start.4) | async-done | bytes 8388640 | tf_op jit(solution)/shard_map/all_to_all | solution.py:40
  984.9 19.0 %copy.58 = bf16[4,64,32,2,256]{4,2,3,1,0:T(8,128)(2,1)} copy(bf16[4,64,32,2,256]{1,4,3,2,0:T(8,128)(2,1)} %bitcast.116) | data formatting | bytes 16777216 | tf_op jit(solution)/shard_map/all_to_all | solution.py:40
  1014.1 29.1 %copy.59 = bf16[4,64,32,512]{1,2,0,3:T(8,128)(2,1)} copy(bf16[4,64,32,512]{3,2,1,0:T(8,128)(2,1)} %bitcast_convert_fusion) | data formatting | bytes 16777216 | tf_op jit(solution)/shard_map/convert_element_type | solution.py:41
  1060.0 99.9 %all_to_all.100 = bf16[4,2,524288]{2,1,0:T(2,128)(2,1)} all-to-all(bf16[4,2,524288]{2,1,0:T(2,128)(2,1)} %reshape.234), channel_id=1, replica_groups=mesh['member'=1,'lon'=4,'lat'=8] {'lon'}, dimensions={0} | all-to-all | bytes 16777216 | tf_op jit(solution)/shard_map/all_to_all | solution.py:42
  1175.9 18.8 %convert_bitcast_fusion = f32[4,4,64,32,128]{2,3,0,4,1:T(8,128)} fusion(bf16[4,64,32,4,128]{1,2,0,4,3:T(8,128)(2,1)} %bitcast.103), kind=kLoop, calls=%fused_computation.5 | loop fusion | flops 4194304 | bytes 25165824 | tf_op jit(solution)/shard_map/convert_element_type | solution.py:43
  1194.7 29.4 %copy.60 = f32[4,4,64,32,128]{4,3,2,1,0:T(8,128)} copy(f32[4,4,64,32,128]{2,3,0,4,1:T(8,128)} %convert_bitcast_fusion) | data formatting | bytes 33554432 | tf_op jit(solution)/shard_map/convert_element_type | solution.py:43
  1224.1 17.0 %fusion.10 = f32[4,256,32,128]{3,2,1,0:T(8,128)} fusion(f32[4,256,32,128]{3,2,1,0:T(8,128)} %param.4, f32[4,256,32,128]{3,2,1,0:T(8,128)} %bitcast.102), kind=kLoop, calls=%fused_computation.14 | loop fusion | flops 37748736 | bytes 50331648 | tf_op jit(solution)/shard_map/add | solution.py:43
  (34 shorter events, 300.8 us)
Async XLA Ops:
  9.6 101.0 %all-to-all-start = ((bf16[4,256,32,128]{3,2,0,1:T(8,128)(2,1)}), bf16[4,256,32,128]{3,2,0,1:T(8,128)(2,1)}, u32[]{:S(2)}, u32[]{:S(2)}) async-start(bf16[4,256,32,128]{3,2,0,1:T(8,128)(2,1)} %copy.81), calls=%async_computation | async-start | bytes 16777216 | tf_op jit(solution)/shard_map/all_to_all | solution.py:28
  169.9 23.4 %copy-start.1 = (u32[32]{0:T(128)S(1)}, u32[32]{0:T(128)}, u32[]{:S(2)}) copy-start(u32[32]{0:T(128)} %constant.31) | copy-start | bytes 388
  186.7 100.0 %all-to-all-start.1 = ((bf16[8,2,262144]{2,1,0:T(2,128)(2,1)}), bf16[8,2,262144]{2,1,0:T(2,128)(2,1)}, u32[]{:S(2)}, u32[]{:S(2)}) async-start(bf16[8,2,262144]{2,1,0:T(2,128)(2,1)} %reshape.226), calls=%async_computation.1 | async-start | bytes 16777216 | tf_op jit(solution)/shard_map/all_to_all | solution.py:30
  380.8 22.8 %copy-start = (u32[32]{0:T(128)S(1)}, u32[32]{0:T(128)}, u32[]{:S(2)}) copy-start(u32[32]{0:T(128)} %constant.39) | copy-start | bytes 388
  397.9 98.1 %all-to-all-start.2 = ((bf16[4,2,524288]{2,1,0:T(2,128)(2,1)}), bf16[4,2,524288]{2,1,0:T(2,128)(2,1)}, u32[]{:S(2)}, u32[]{:S(2)}) async-start(bf16[4,2,524288]{2,1,0:T(2,128)(2,1)} %reshape.228), calls=%async_computation.2 | async-start | bytes 16777216 | tf_op jit(solution)/shard_map/all_to_all | solution.py:32
  848.3 101.9 %all-to-all-start.4 = ((bf16[8,2,262144]{2,1,0:T(2,128)(2,1)}), bf16[8,2,262144]{2,1,0:T(2,128)(2,1)}, u32[]{:S(2)}, u32[]{:S(2)}) async-start(bf16[8,2,262144]{2,1,0:T(2,128)(2,1)} %reshape.232), calls=%async_computation.4 | async-start | bytes 16777216 | tf_op jit(solution)/shard_map/all_to_all | solution.py:40
where the time goes:
time: 1260 us; the launch traced here: 1240 us
  local copies, waits for them, and re-layouts  559 us (44%)
  waiting for transfers between devices  310 us (25%)
  blocking collectives  199 us (16%)
  matrix products  75.1 us (6%)
  other arithmetic  69.8 us (6%)
  starting transfers between devices  27.2 us (2%)
    unnamed x16, local copies, waits for them, and re-layouts  185 us
    all_to_all x1, blocking collectives, local_layer(): wave_grid = lax.all_to_all(wave_loc, 'lon', 3, 1, tiled=True)  99.9 us
    all_to_all x1, blocking collectives, local_layer(): mixed_loc = lax.all_to_all(mixed_chan, 'lon', 1, 2, tiled=True)  98.6 us
    all_to_all x1, waiting for transfers between devices, local_layer(): lon_full = lax.all_to_all(grid_bf, 'lon', 1, 3, tiled=True)  92.3 us
    all_to_all x1, waiting for transfers between devices, local_layer(): spec_loc = lax.all_to_all(spec_all, 'lat', 4, 2, tiled=True)  92.2 us
    all_to_all x1, waiting for transfers between devices, local_layer(): back_all = lax.all_to_all(back_loc, 'lat', 2, 4, tiled=True)  89.4 us
    all_to_all x2, local copies, waits for them, and re-layouts, local_layer(): mixed_loc = lax.all_to_all(mixed_chan, 'lon', 1, 2, tiled=True)  46.5 us
    all_to_all x2, local copies, waits for them, and re-layouts, local_layer(): coef_chan = lax.all_to_all(coef_loc, 'lon', 2, 1, tiled=True)  44.3 us
  transfers between devices with their start and end apart: 4, of which 4 were waited for; matrix products, arithmetic and copies ran while one was open for 5% of the time, Pallas kernels for 0%

commit v1 on v0

v1 whole, which is shorter than its diff:
```python
import functools
import math
import jax
import jax.numpy as jnp
from jax import lax
from jax.experimental import pallas as pl
from jax.experimental.pallas import tpu as pltpu
from jax.sharding import PartitionSpec as P

MESH = pl.DeviceIdType.MESH
ROWS = 16
LANES = 128
VMEM_LIMIT = 66000000


def row_waves(degrees, lat_count):
    m_loc = degrees // lat_count
    groups = m_loc // ROWS
    waves = jnp.arange(degrees).reshape(lat_count, groups, 1, ROWS)
    waves = jnp.broadcast_to(waves, (lat_count, groups, 2, ROWS)).reshape(-1)
    part = jnp.broadcast_to(jnp.arange(2).reshape(1, 1, 2, 1), (lat_count, groups, 2, ROWS)).reshape(-1)
    return waves, part


def dft_tables(lon_points, degrees, lat_count):
    waves, part = row_waves(degrees, lat_count)
    lon_ids = jnp.arange(lon_points)
    arg = (2.0 * math.pi / lon_points) * ((waves[:, None] * lon_ids[None, :]) % lon_points).astype(jnp.float32)
    value = jnp.where(part[:, None] == 0, jnp.cos(arg), -jnp.sin(arg))
    weight = jnp.where(waves == 0, 1.0, 2.0).astype(jnp.float32)
    return value.astype(jnp.bfloat16), (weight[:, None] * value).astype(jnp.bfloat16)


def entry_barrier(lon_count, lat_count):
    k, d = lax.axis_index('lon'), lax.axis_index('lat')
    sem = pltpu.get_barrier_semaphore()
    for q in range(1, lon_count):
        pl.semaphore_signal(sem, inc=1, device_id={'lon': lax.rem(k + q, lon_count)}, device_id_type=MESH)
    for e in range(1, lat_count):
        pl.semaphore_signal(sem, inc=1, device_id={'lat': lax.rem(d + e, lat_count)}, device_id_type=MESH)
    pl.semaphore_wait(sem, lon_count - 1 + lat_count - 1)


def lat_order(lat_count):
    order = [e for pair in zip(range(2, lat_count, 1), range(lat_count - 2, 0, -1)) for e in pair]
    order = list(dict.fromkeys(order))
    return order + [e for e in range(1, lat_count) if e not in order]


def lon_order(lon_count):
    order = []
    for q in range(1, lon_count // 2 + 1):
        order += [q, lon_count - q]
    return list(dict.fromkeys(order))


def to_spectral_kernel(lon_count, lat_count, t_loc, x_ref, dft_ref, out_ref, xin, xs, xr, stage, fb,
                       load_sem, y_send, y_recv, x_send, x_recv, keep_sem):
    k, d = lax.axis_index('lon'), lax.axis_index('lat')
    samples = x_ref.shape[0]
    channels = x_ref.shape[1] // t_loc
    halves, t_groups = channels // LANES, t_loc // ROWS
    rows = fb.shape[1]
    half_rows = LANES * t_loc

    loads = []
    for h in range(halves):
        for q in range(samples):
            src_s = lax.rem(k + q, lon_count)
            part = pl.ds(h * half_rows, half_rows)
            loads.append(pltpu.make_async_copy(x_ref.at[src_s, part], xin.at[q, part], load_sem.at[h, q]))
    for copy in loads:
        copy.start()
    entry_barrier(lon_count, lat_count)

    chunks = [(h, g) for h in range(halves) for g in range(t_groups)]
    y_copies = []
    for n, (h, g) in enumerate(chunks):
        sent = {}
        for q in lon_order(lon_count) + [0]:
            if g == 0:
                loads[h * samples + q].wait()

            def narrow(i, carry, q=q, h=h, g=g):
                t = g * ROWS + i
                block = xin[q, pl.ds(h * half_rows + t, LANES, stride=t_loc), :].astype(jnp.bfloat16)
                if q == 0:
                    xr[k, t, pl.ds(h * LANES, LANES), :] = block
                else:
                    xs[q - 1, t, pl.ds(h * LANES, LANES), :] = block
                return carry

            lax.fori_loop(0, ROWS, narrow, 0)
            if q:
                part = (pl.ds(g * ROWS, ROWS), pl.ds(h * LANES, LANES))
                sent[q] = pltpu.make_async_remote_copy(
                    src_ref=xs.at[(q - 1,) + part], dst_ref=xr.at[(k,) + part],
                    send_sem=y_send.at[n, q - 1], recv_sem=y_recv.at[n, q - 1],
                    device_id={'lon': lax.rem(k + q, lon_count)}, device_id_type=MESH)
                sent[q].start()
        y_copies.append(sent)

    kept, x_copies = [], []
    for n, (h, g) in enumerate(chunks):
        for q in range(1, lon_count):
            y_copies[n][q].wait_recv()

        def transform(i, carry, h=h, g=g):
            t = g * ROWS + i
            cols = jnp.concatenate([xr[b, t, pl.ds(h * LANES, LANES), :] for b in range(lon_count)], axis=1)
            spec = lax.dot_general(dft_ref[...], cols, (((1,), (1,)), ((), ())), preferred_element_type=jnp.float32)
            stage[pl.ds(i, lat_count * rows, stride=ROWS), :] = spec
            return carry

        lax.fori_loop(0, ROWS, transform, 0)
        for e in lat_order(lat_count) + [0]:
            dd = lax.rem(d + e, lat_count)

            def pack(r, carry, e=e, dd=dd, h=h, g=g):
                first = pl.multiple_of(dd * (rows * ROWS) + r * (8 * ROWS), ROWS)
                block = stage[pl.ds(first, 8 * ROWS), :].astype(jnp.bfloat16)
                fb[e, pl.ds(r * 8, 8), pl.ds(g * ROWS, ROWS), pl.ds(h * LANES, LANES)] = block.reshape(8, ROWS, LANES)
                return carry

            lax.fori_loop(0, rows // 8, pack, 0)
            src = fb.at[e, :, pl.ds(g * ROWS, ROWS), pl.ds(h * LANES, LANES)]
            dst = out_ref.at[:, pl.ds(pl.multiple_of(d * t_loc + g * ROWS, ROWS), ROWS), pl.ds(h * LANES, LANES)]
            if e == 0:
                copy = pltpu.make_async_copy(src, dst, keep_sem.at[n])
                kept.append(copy)
            else:
                copy = pltpu.make_async_remote_copy(
                    src_ref=src, dst_ref=dst, send_sem=x_send.at[n, e - 1], recv_sem=x_recv.at[n, e - 1],
                    device_id={'lat': dd}, device_id_type=MESH)
                x_copies.append(copy)
            copy.start()
    for sent in y_copies:
        for q in range(1, lon_count):
            sent[q].wait_send()
    for copy in kept:
        copy.wait()
    for copy in x_copies:
        copy.wait_send()
        copy.wait_recv()


def to_grid_kernel(lon_count, lat_count, t_loc, g_ref, dft_ref, out_ref, gr, stage, ys,
                   load_sem, x_send, x_recv, y_send, y_recv, keep_sem):
    k, d = lax.axis_index('lon'), lax.axis_index('lat')
    rows, channels = g_ref.shape[1], g_ref.shape[2]
    halves, t_groups = channels // LANES, t_loc // ROWS
    entry_barrier(lon_count, lat_count)
    chunks = [(h, g) for h in range(halves) for g in range(t_groups)]
    own, x_copies = [], []
    for n, (h, g) in enumerate(chunks):
        sent = []
        for e in lat_order(lat_count) + [0]:
            dd = lax.rem(d + e, lat_count)
            src = g_ref.at[pl.ds(dd * t_loc + g * ROWS, ROWS), :, pl.ds(h * LANES, LANES)]
            dst = gr.at[pl.ds(g * ROWS, ROWS), pl.ds(pl.multiple_of(d * rows, ROWS), rows), pl.ds(h * LANES, LANES)]
            if e == 0:
                copy = pltpu.make_async_copy(src, dst, load_sem.at[n])
                own.append(copy)
            else:
                copy = pltpu.make_async_remote_copy(
                    src_ref=src, dst_ref=dst, send_sem=x_send.at[n, e - 1], recv_sem=x_recv.at[n, e - 1],
                    device_id={'lat': dd}, device_id_type=MESH)
                sent.append(copy)
            copy.start()
        x_copies.append(sent)

    kept, y_copies = [], []
    for n, (h, g) in enumerate(chunks):
        own[n].wait()
        for copy in x_copies[n]:
            copy.wait_recv()

        def transform(i, carry, h=h, g=g):
            spec = gr[g * ROWS + i, :, pl.ds(h * LANES, LANES)]
            wave = lax.dot_general(spec, dft_ref[...], (((0,), (0,)), ((), ())), preferred_element_type=jnp.float32)
            for b in range(lon_count):
                stage[b, pl.ds(i, LANES, stride=ROWS), :] = wave[:, b * LANES:(b + 1) * LANES]
            return carry

        lax.fori_loop(0, ROWS, transform, 0)
        for q in lon_order(lon_count) + [0]:
            kk = lax.rem(k + q, lon_count)

            def pack(r, carry, q=q, kk=kk, h=h, g=g):
                block = stage[kk, pl.ds(pl.multiple_of(r * (8 * ROWS), ROWS), 8 * ROWS), :].astype(jnp.bfloat16)
                ys[q, pl.ds(h * LANES + r * 8, 8), pl.ds(g * ROWS, ROWS), :] = block.reshape(8, ROWS, LANES)
                return carry

            lax.fori_loop(0, LANES // 8, pack, 0)
            part = (pl.ds(h * LANES, LANES), pl.ds(g * ROWS, ROWS))
            src, dst = ys.at[(q,) + part], out_ref.at[(k,) + part]
            if q == 0:
                copy = pltpu.make_async_copy(src, dst, keep_sem.at[n])
                kept.append(copy)
            else:
                copy = pltpu.make_async_remote_copy(
                    src_ref=src, dst_ref=dst, send_sem=y_send.at[n, q - 1], recv_sem=y_recv.at[n, q - 1],
                    device_id={'lon': kk}, device_id_type=MESH)
                y_copies.append(copy)
            copy.start()
    for sent in x_copies:
        for copy in sent:
            copy.wait_send()
    for copy in kept:
        copy.wait()
    for copy in y_copies:
        copy.wait_send()
        copy.wait_recv()


def legendre_kernel(transposed, base_ref, table_ref, in_ref, out_ref, stage):
    i = pl.program_id(1)
    table = table_ref[0].astype(jnp.bfloat16)
    dims = (((0,), (0,)), ((), ())) if transposed else (((1,), (0,)), ((), ()))
    size = out_ref.shape[0]
    halves = in_ref.shape[4] // LANES
    for r in range(2):
        res = lax.dot_general(table, in_ref[0, r, 0], dims, preferred_element_type=jnp.float32)
        for h in range(halves):
            stage[r, h, pl.ds(i, size, stride=ROWS), :] = res[:, h * LANES:(h + 1) * LANES]

    @pl.when(i == ROWS - 1)
    def _():
        def pack(n, carry):
            for r in range(2):
                for h in range(halves):
                    block = stage[r, h, pl.ds(pl.multiple_of(n * (8 * ROWS), ROWS), 8 * ROWS), :].astype(jnp.bfloat16)
                    out_ref[pl.ds(n * 8, 8), pl.ds(r * ROWS, ROWS), pl.ds(h * LANES, LANES)] = block.reshape(8, ROWS, LANES)
            return carry

        lax.fori_loop(0, size // 8, pack, 0)


def legendre(table, values, base, transposed):
    groups, _, _, length, channels = values.shape
    size = table.shape[2] if transposed else table.shape[1]
    return pl.pallas_call(
        functools.partial(legendre_kernel, transposed),
        out_shape=jax.ShapeDtypeStruct((size, groups * 2 * ROWS, channels), jnp.bfloat16),
        grid_spec=pltpu.PrefetchScalarGridSpec(
            num_scalar_prefetch=1, grid=(groups, ROWS),
            in_specs=[
                pl.BlockSpec((1,) + table.shape[1:], lambda g, i, base_ref: (base_ref[0] + g * ROWS + i, 0, 0)),
                pl.BlockSpec((1, 2, 1, length, channels), lambda g, i, base_ref: (g, 0, i, 0, 0)),
            ],
            out_specs=pl.BlockSpec((size, 2 * ROWS, channels), lambda g, i, base_ref: (0, g, 0)),
            scratch_shapes=[pltpu.VMEM((2, channels // LANES, size * ROWS, LANES), jnp.float32)]),
        compiler_params=pltpu.CompilerParams(vmem_limit_bytes=VMEM_LIMIT),
        name='legendre_back' if transposed else 'legendre_fwd',
    )(base, table, values)


def mix_kernel(w_ref, a_ref, out_ref, stage):
    rows, channels = a_ref.shape[1], a_ref.shape[2]
    tiles = channels // LANES
    stride = 2 * tiles

    def degree(n, carry):
        def weight(r):
            pieces = [w_ref[pl.ds(n * channels * stride + 2 * b + r, channels, stride=stride), :] for b in range(tiles)]
            return jnp.concatenate([p.astype(jnp.bfloat16) for p in pieces], axis=1)

        val = a_ref[n]
        turned = []
        for first in range(0, rows, 2 * ROWS):
            turned += [-val[first + ROWS:first + 2 * ROWS], val[first:first + ROWS]]
        turned = jnp.concatenate(turned, axis=0)
        dims = (((1,), (1,)), ((), ()))
        res = lax.dot_general(val, weight(0), dims, preferred_element_type=jnp.float32)
        res = res + lax.dot_general(turned, weight(1), dims, preferred_element_type=jnp.float32)
        for h in range(tiles):
            stage[h, pl.ds(n, rows, stride=ROWS), :] = res[:, h * LANES:(h + 1) * LANES]
        return carry

    lax.fori_loop(0, ROWS, degree, 0)
    for h in range(tiles):
        out_ref[:, :, h * LANES:(h + 1) * LANES] = stage[h].astype(jnp.bfloat16).reshape(rows, ROWS, LANES)


def mix(w_rows, coef):
    degrees, rows, channels = coef.shape
    per_degree = w_rows.shape[0] // degrees
    return pl.pallas_call(
        mix_kernel,
        out_shape=jax.ShapeDtypeStruct((rows, degrees, channels), jnp.bfloat16),
        grid=(degrees // ROWS,),
        in_specs=[
            pl.BlockSpec((ROWS * per_degree, LANES), lambda n: (n, 0)),
            pl.BlockSpec((ROWS, rows, channels), lambda n: (n, 0, 0)),
        ],
        out_specs=pl.BlockSpec((rows, ROWS, channels), lambda n: (0, n, 0)),
        scratch_shapes=[pltpu.VMEM((channels // LANES, rows * ROWS, LANES), jnp.float32)],
        compiler_params=pltpu.CompilerParams(vmem_limit_bytes=VMEM_LIMIT),
        name='mix',
    )(w_rows, coef)


def solution(mesh):
    lon_count, lat_count = mesh.shape['lon'], mesh.shape['lat']
    grid_spec = P('member', None, 'lat', 'lon')
    any_spec = pl.BlockSpec(memory_space=pl.ANY)
    vmem_spec = pl.BlockSpec(memory_space=pltpu.VMEM)
    dma = pltpu.SemaphoreType.DMA

    def local_layer(field_in, fwd_table, inv_table, mix_weights):
        samples, channels, t_loc, j_loc = field_in.shape
        degrees, latitudes = fwd_table.shape[1], fwd_table.shape[2]
        lon_points = j_loc * lon_count
        m_loc = degrees // lat_count
        groups, rows = m_loc // ROWS, 2 * m_loc
        n_chunks = (channels // LANES) * (t_loc // ROWS)
        fwd_dft, inv_dft = dft_tables(lon_points, degrees, lat_count)
        base = (lax.axis_index('lat') * m_loc).astype(jnp.int32).reshape(1)

        spec = pl.pallas_call(
            functools.partial(to_spectral_kernel, lon_count, lat_count, t_loc),
            out_shape=jax.ShapeDtypeStruct((rows, latitudes, channels), jnp.bfloat16),
            in_specs=[any_spec, vmem_spec],
            out_specs=any_spec,
            scratch_shapes=[
                pltpu.VMEM((samples, channels * t_loc, j_loc), jnp.float32),
                pltpu.VMEM((samples - 1, t_loc, channels, j_loc), jnp.bfloat16),
                pltpu.VMEM((lon_count, t_loc, channels, j_loc), jnp.bfloat16),
                pltpu.VMEM((lat_count * rows * ROWS, LANES), jnp.float32),
                pltpu.VMEM((lat_count, rows, t_loc, channels), jnp.bfloat16),
                dma((channels // LANES, samples)),
                dma((n_chunks, lon_count - 1)), dma((n_chunks, lon_count - 1)),
                dma((n_chunks, lat_count - 1)), dma((n_chunks, lat_count - 1)),
                dma((n_chunks,)),
            ],
            compiler_params=pltpu.CompilerParams(collective_id=0, has_side_effects=True, vmem_limit_bytes=VMEM_LIMIT),
            name='to_spectral',
        )(field_in.reshape(samples, channels * t_loc, j_loc), fwd_dft)

        coef = legendre(fwd_table, spec.reshape(groups, 2, ROWS, latitudes, channels), base, False)
        w_rows = mix_weights.reshape(degrees, channels, channels // LANES, LANES, 2)
        w_rows = jnp.transpose(w_rows, (0, 1, 2, 4, 3)).reshape(-1, LANES)
        mixed = mix(w_rows, coef)
        back = legendre(inv_table, mixed.reshape(groups, 2, ROWS, degrees, channels), base, True)

        wave = pl.pallas_call(
            functools.partial(to_grid_kernel, lon_count, lat_count, t_loc),
            out_shape=jax.ShapeDtypeStruct((samples, channels, t_loc, j_loc), jnp.bfloat16),
            in_specs=[any_spec, vmem_spec],
            out_specs=any_spec,
            scratch_shapes=[
                pltpu.VMEM((t_loc, lat_count * rows, channels), jnp.bfloat16),
                pltpu.VMEM((lon_count, LANES * ROWS, LANES), jnp.float32),
                pltpu.VMEM((lon_count, channels, t_loc, j_loc), jnp.bfloat16),
                dma((n_chunks,)),
                dma((n_chunks, lat_count - 1)), dma((n_chunks, lat_count - 1)),
                dma((n_chunks, lon_count - 1)), dma((n_chunks, lon_count - 1)),
                dma((n_chunks,)),
            ],
            compiler_params=pltpu.CompilerParams(collective_id=1, has_side_effects=True, vmem_limit_bytes=VMEM_LIMIT),
            name='to_grid',
        )(back, inv_dft)
        return field_in + jax.nn.gelu(wave.astype(jnp.float32), approximate=True)

    whole = P(None, None, None)
    return jax.shard_map(local_layer, mesh=mesh, in_specs=(grid_spec, whole, whole, P(None, None, None, None)),
                         out_specs=grid_spec, check_vma=False)
```

time: 1260 us -> 402 us (0.32); the launches traced: 1240 us -> 400 us
  local copies, waits for them, and re-layouts: 559 us -> 0.19 us
  Pallas kernels: 0 us -> 379 us
  waiting for transfers between devices: 310 us -> 0 us
  blocking collectives: 199 us -> 0 us
  matrix products: 75.1 us -> 0 us
  other arithmetic: 69.8 us -> 21.2 us
  starting transfers between devices: 27.2 us -> 0 us
    pallas_call x0 -> x5, Pallas kernels: none -> 379 us  [the longest x1 133 us: local_layer(): pl.pallas_call(functools.partial(to_spectral_kernel, lon_count, lat_count...]
    all_to_all x4 -> x0, waiting for transfers between devices: 310 us -> none  [the longest x1 92.3 us: local_layer(): lon_full = lax.all_to_all(grid_bf, 'lon', 1, 3, tiled=True)]
    all_to_all x2 -> x0, blocking collectives: 199 us -> none  [the longest x1 99.9 us: local_layer(): wave_grid = lax.all_to_all(wave_loc, 'lon', 3, 1, tiled=True)]
    unnamed x16 -> x0, local copies, waits for them, and re-layouts: 185 us -> none
    convert_element_type x6 -> x0, local copies, waits for them, and re-layouts: 184 us -> none  [the longest x1 36.1 us: local_layer(): jnp.einsum('mlt,sctrm->sclrm', fwd_table.astype(jnp.bfloat16), spec_loc,...]
    all_to_all x10 -> x0, local copies, waits for them, and re-layouts: 172 us -> none  [the longest x2 46.5 us: local_layer(): mixed_loc = lax.all_to_all(mixed_chan, 'lon', 1, 2, tiled=True)]
    dot_general x5 -> x0, matrix products: 75.1 us -> none  [the longest x1 22.7 us: local_layer(): jnp.einsum('mlt,sctrm->sclrm', fwd_table.astype(jnp.bfloat16), spec_loc,...]
    another operation x4 -> x0, other arithmetic: 27.7 us -> none  [the longest x1 21.4 us: local_layer(): jnp.stack([jnp.stack([w_re, -w_im], axis=-1), jnp.stack([w_im, w_re], axi...]
  transfers between devices with their start and end apart: 4 -> 0, of which waited for: 4 -> 0; matrix products, arithmetic and copies ran while one was open for 5% -> 0% of each run, Pallas kernels for 0% -> 0%
where the time goes in v1:
time: 402 us; the launch traced here: 400 us
  Pallas kernels  379 us (94%)
  other arithmetic  21.2 us (5%)
    pallas_call x1, Pallas kernels, local_layer(): pl.pallas_call(functools.partial(to_spectral_kernel, lon_count, lat_count...  133 us
    pallas_call x1, Pallas kernels, local_layer(): pl.pallas_call(functools.partial(to_grid_kernel, lon_count, lat_count, t_...  125 us
    pallas_call x1, Pallas kernels, mix(): pl.pallas_call(mix_kernel, out_shape=jax.ShapeDtypeStruct((rows, degrees,...  62 us
    pallas_call x2, Pallas kernels, legendre(): pl.pallas_call(functools.partial(legendre_kernel, transposed), out_shape=...  58.7 us
    add x1, other arithmetic, local_layer(): return field_in + jax.nn.gelu(wave.astype(jnp.float32), approximate=True)  15.4 us

profile of v1, /device:TPU:97, one launch (start us, length us, event | category | flops | bytes accessed | tf_op | source)
XLA Modules:
  0.0 400.2 jit_solution(2329454139136508085)
XLA Ops:
  0.0 0.1 mul.64
  0.1 0.1 eq.32
  0.2 5.8 %multiply_convert_fusion = (bf16[512,512]{1,0:T(8,128)(2,1)}, bf16[512,512]{1,0:T(8,128)(2,1)}) fusion(f32[512]{0:T(512)S(1)} %compare_select_fusion, s32[512]{0:T(512)S(1)} %mul.64, pred[512]{0:T(512)(128)(4,1)S(1)} %eq.32), kind=kLoop, calls=%fused_computation.16 | loop fusion | flops 4980736 | bytes 1053184 | tf_op jit(solution)/shard_map/convert_element_type | solution.py:31
  6.0 132.8 %to_spectral.1 = bf16[64,256,256]{2,1,0:T(8,128)(2,1)} custom-call(f32[4,8192,128]{2,1,0:T(8,128)} %bitcast.9, bf16[512,512]{1,0:T(8,128)(2,1)} %get-tuple-element.6.dft_ref), custom_call_target="tpu_custom_call" | custom-call | tf_op jit(solution)/shard_map/to_spectral/pallas_call | solution.py:320
  138.8 29.4 %legendre_fwd.1.a_ref = bf16[256,64,256]{2,1,0:T(8,128)(2,1)} custom-call(s32[1]{0:T(128)} %bitcast.base_ref, f32[256,256,256]{2,1,0:T(8,128)} %table_ref.2, bf16[2,2,16,256,256]{4,3,2,1,0:T(8,128)(2,1)} %bitcast.11), custom_call_target="tpu_custom_call" | custom-call | tf_op jit(solution)/shard_map/legendre_fwd/pallas_call | solution.py:242
  168.2 62.0 %mix.1 = bf16[64,256,256]{2,1,0:T(8,128)(2,1)} custom-call(f32[262144,128]{1,0:T(8,128)} %bitcast.3.w_ref, bf16[256,64,256]{2,1,0:T(8,128)(2,1)} %legendre_fwd.1.a_ref), custom_call_target="tpu_custom_call" | custom-call | tf_op jit(solution)/shard_map/mix/pallas_call | solution.py:288
  230.2 29.2 %legendre_back.1.g_ref = bf16[256,64,256]{2,1,0:T(8,128)(2,1)} custom-call(s32[1]{0:T(128)} %bitcast.base_ref, f32[256,256,256]{2,1,0:T(8,128)} %table_ref.3, bf16[2,2,16,256,256]{4,3,2,1,0:T(8,128)(2,1)} %bitcast.10), custom_call_target="tpu_custom_call" | custom-call | tf_op jit(solution)/shard_map/legendre_back/pallas_call | solution.py:242
  259.5 125.3 %to_grid.1 = bf16[4,256,32,128]{3,2,1,0:T(8,128)(2,1)} custom-call(bf16[256,64,256]{2,1,0:T(8,128)(2,1)} %legendre_back.1.g_ref, bf16[512,512]{1,0:T(8,128)(2,1)} %get-tuple-element.5.dft_ref), custom_call_target="tpu_custom_call" | custom-call | tf_op jit(solution)/shard_map/to_grid/pallas_call | solution.py:346
  384.8 15.4 %fusion.5 = f32[4,256,32,128]{3,2,1,0:T(8,128)} fusion(f32[4,256,32,128]{3,2,1,0:T(8,128)} %param.4, bf16[4,256,32,128]{3,2,1,0:T(8,128)(2,1)} %to_grid.1), kind=kLoop, calls=%fused_computation.9 | loop fusion | flops 41943040 | bytes 41943040 | tf_op jit(solution)/shard_map/add | solution.py:363
  (4 shorter events, 0.0 us)

commit v2 on v1

v2 whole, which is shorter than its diff:
```python
import functools
import math
import jax
import jax.numpy as jnp
from jax import lax
from jax.experimental import pallas as pl
from jax.experimental.pallas import tpu as pltpu
from jax.sharding import PartitionSpec as P

MESH = pl.DeviceIdType.MESH
ROWS = 16
T_ROWS = 8
PITCH = 17
WAVES = 4
LANES = 128
VMEM_LIMIT = 66000000


def row_waves(degrees, lat_count):
    m_loc = degrees // lat_count
    groups = m_loc // ROWS
    waves = jnp.arange(degrees).reshape(lat_count, groups, 1, ROWS)
    waves = jnp.broadcast_to(waves, (lat_count, groups, 2, ROWS)).reshape(-1)
    part = jnp.broadcast_to(jnp.arange(2).reshape(1, 1, 2, 1), (lat_count, groups, 2, ROWS)).reshape(-1)
    return waves, part


def dft_tables(lon_points, degrees, lat_count):
    waves, part = row_waves(degrees, lat_count)
    lon_ids = jnp.arange(lon_points)
    arg = (2.0 * math.pi / lon_points) * ((waves[:, None] * lon_ids[None, :]) % lon_points).astype(jnp.float32)
    value = jnp.where(part[:, None] == 0, jnp.cos(arg), -jnp.sin(arg))
    weight = jnp.where(waves == 0, 1.0, 2.0).astype(jnp.float32)
    return value.astype(jnp.bfloat16), (weight[:, None] * value).astype(jnp.bfloat16)


def entry_barrier(lon_count, lat_count):
    k, d = lax.axis_index('lon'), lax.axis_index('lat')
    sem = pltpu.get_barrier_semaphore()
    for q in range(1, lon_count):
        pl.semaphore_signal(sem, inc=1, device_id={'lon': lax.rem(k + q, lon_count)}, device_id_type=MESH)
    for e in range(1, lat_count):
        pl.semaphore_signal(sem, inc=1, device_id={'lat': lax.rem(d + e, lat_count)}, device_id_type=MESH)
    pl.semaphore_wait(sem, lon_count - 1 + lat_count - 1)


def lat_order(lat_count):
    order = [e for pair in zip(range(2, lat_count, 1), range(lat_count - 2, 0, -1)) for e in pair]
    order = list(dict.fromkeys(order))
    return order + [e for e in range(1, lat_count) if e not in order]


def lon_order(lon_count):
    order = []
    for q in range(1, lon_count // 2 + 1):
        order += [q, lon_count - q]
    return list(dict.fromkeys(order))


def to_spectral_kernel(lon_count, lat_count, t_loc, x_ref, dft_ref, out_ref, xin, xs, xr, stage, fb,
                       load_sem, y_send, y_recv, x_send, x_recv, keep_sem):
    k, d = lax.axis_index('lon'), lax.axis_index('lat')
    samples = x_ref.shape[0]
    channels = x_ref.shape[1] // t_loc
    halves, t_groups = channels // LANES, t_loc // T_ROWS
    rows = fb.shape[1]
    half_rows = LANES * t_loc

    loads = []
    for h in range(halves):
        for q in range(samples):
            src_s = lax.rem(k + q, lon_count)
            part = pl.ds(h * half_rows, half_rows)
            loads.append(pltpu.make_async_copy(x_ref.at[src_s, part], xin.at[q, part], load_sem.at[h, q]))
    for copy in loads:
        copy.start()
    entry_barrier(lon_count, lat_count)

    chunks = [(h, g) for h in range(halves) for g in range(t_groups)]
    y_copies = []
    for n, (h, g) in enumerate(chunks):
        sent = {}
        for q in lon_order(lon_count) + [0]:
            if g == 0:
                loads[h * samples + q].wait()

            def narrow(i, carry, q=q, h=h, g=g):
                t = g * T_ROWS + i
                block = xin[q, pl.ds(h * half_rows + t, LANES, stride=t_loc), :].astype(jnp.bfloat16)
                if q == 0:
                    xr[k, t, pl.ds(h * LANES, LANES), :] = block
                else:
                    xs[q - 1, t, pl.ds(h * LANES, LANES), :] = block
                return carry

            lax.fori_loop(0, T_ROWS, narrow, 0)
            if q:
                part = (pl.ds(g * T_ROWS, T_ROWS), pl.ds(h * LANES, LANES))
                sent[q] = pltpu.make_async_remote_copy(
                    src_ref=xs.at[(q - 1,) + part], dst_ref=xr.at[(k,) + part],
                    send_sem=y_send.at[n, q - 1], recv_sem=y_recv.at[n, q - 1],
                    device_id={'lon': lax.rem(k + q, lon_count)}, device_id_type=MESH)
                sent[q].start()
        y_copies.append(sent)

    kept, x_copies = [], []
    for n, (h, g) in enumerate(chunks):
        for q in range(1, lon_count):
            y_copies[n][q].wait_recv()

        def transform(i, carry, h=h, g=g):
            t = g * T_ROWS + i
            cols = jnp.concatenate([xr[b, t, pl.ds(h * LANES, LANES), :] for b in range(lon_count)], axis=1)
            spec = lax.dot_general(dft_ref[...], cols, (((1,), (1,)), ((), ())), preferred_element_type=jnp.float32)
            stage[pl.ds(i, lat_count * rows, stride=T_ROWS), :] = spec
            return carry

        lax.fori_loop(0, T_ROWS, transform, 0)
        for e in lat_order(lat_count) + [0]:
            dd = lax.rem(d + e, lat_count)

            def pack(r, carry, e=e, dd=dd, h=h, g=g):
                first = pl.multiple_of(dd * (rows * T_ROWS) + r * (8 * T_ROWS), T_ROWS)
                block = stage[pl.ds(first, 8 * T_ROWS), :].reshape(8, T_ROWS, LANES)
                fb[e, pl.ds(r * 8, 8), pl.ds(g * T_ROWS, T_ROWS), pl.ds(h * LANES, LANES)] = block.astype(jnp.bfloat16)
                return carry

            lax.fori_loop(0, rows // 8, pack, 0)
            src = fb.at[e, :, pl.ds(g * T_ROWS, T_ROWS), pl.ds(h * LANES, LANES)]
            dst = out_ref.at[:, pl.ds(pl.multiple_of(d * t_loc + g * T_ROWS, T_ROWS), T_ROWS), pl.ds(h * LANES, LANES)]
            if e == 0:
                copy = pltpu.make_async_copy(src, dst, keep_sem.at[n])
                kept.append(copy)
            else:
                copy = pltpu.make_async_remote_copy(
                    src_ref=src, dst_ref=dst, send_sem=x_send.at[n, e - 1], recv_sem=x_recv.at[n, e - 1],
                    device_id={'lat': dd}, device_id_type=MESH)
                x_copies.append(copy)
            copy.start()
    for sent in y_copies:
        for q in range(1, lon_count):
            sent[q].wait_send()
    for copy in kept:
        copy.wait()
    for copy in x_copies:
        copy.wait_send()
        copy.wait_recv()


def mix_to_grid_kernel(lon_count, lat_count, t_loc, coef_ref, w_ref, table_ref, dft_ref, out_ref,
                       wbuf, abuf, mixed, mstage, tables, lstage, gs, gr, ystage, ys,
                       w_sem, a_sem, table_sem, x_send, x_recv, y_send, y_recv, keep_sem):
    k, d = lax.axis_index('lon'), lax.axis_index('lat')
    degrees, rows, channels = coef_ref.shape
    latitudes, m_loc = table_ref.shape[2], tables.shape[0]
    halves, t_groups, tiles = channels // LANES, t_loc // T_ROWS, channels // LANES
    groups, blocks = m_loc // ROWS, degrees // ROWS
    per_half = LANES * 2 * tiles
    nt = (((1,), (1,)), ((), ()))
    tn = (((0,), (0,)), ((), ()))

    def fetch(n):
        h, b, slot = lax.div(n, blocks), lax.rem(n, blocks), lax.rem(n, 2)
        degs = pl.ds(pl.multiple_of(b * ROWS, ROWS), ROWS)
        part = pl.ds(pl.multiple_of(h * per_half, per_half), per_half)
        return (pltpu.make_async_copy(w_ref.at[degs, part], wbuf.at[slot], w_sem.at[slot]),
                pltpu.make_async_copy(coef_ref.at[degs], abuf.at[slot], a_sem.at[slot]))

    for copy in fetch(0):
        copy.start()
    load_tables = pltpu.make_async_copy(table_ref.at[pl.ds(d * m_loc, m_loc)], tables, table_sem)
    load_tables.start()
    entry_barrier(lon_count, lat_count)

    def mix(h, first, last):
        def block(b, carry):
            n = h * blocks + b
            slot = lax.rem(n, 2)

            @pl.when(n + 1 < halves * blocks)
            def _():
                for copy in fetch(n + 1):
                    copy.start()

            for copy in fetch(n):
                copy.wait()

            def degree(u, carry):
                w = jnp.concatenate([
                    jnp.concatenate([
                        wbuf[slot, u, pl.ds(2 * i + r, LANES, stride=2 * tiles), :].astype(jnp.bfloat16)
                        for i in range(tiles)], axis=1)
                    for r in range(2)], axis=0)
                res = lax.dot_general(abuf[slot, u], w, nt, preferred_element_type=jnp.float32)
                parts = []
                for f in range(0, rows, 2 * ROWS):
                    re, im = res[f:f + ROWS], res[f + ROWS:f + 2 * ROWS]
                    parts += [re[:, :LANES] - im[:, LANES:], im[:, :LANES] + re[:, LANES:]]
                mstage[pl.ds(u, rows, stride=PITCH), :] = jnp.concatenate(parts, axis=0)
                return carry

            lax.fori_loop(0, ROWS, degree, 0, unroll=8)
            degs = pl.ds(pl.multiple_of(b * ROWS, ROWS), ROWS)
            for row in range(rows):
                mixed[row, degs, :] = mstage[row * PITCH:row * PITCH + ROWS, :].astype(jnp.bfloat16)
            return carry

        lax.fori_loop(first, last, block, 0)

    def legendre_back(h):
        lanes = pl.ds(h * LANES, LANES)
        for gi in range(groups):
            def wave(w, carry):
                table = tables[gi * ROWS + w].astype(jnp.bfloat16)
                both = jnp.concatenate([mixed[gi * 2 * ROWS + w], mixed[gi * 2 * ROWS + ROWS + w]], axis=1)
                res = lax.dot_general(table, both, tn, preferred_element_type=jnp.float32)
                for r in range(2):
                    lstage[r, pl.ds(w, latitudes, stride=PITCH), :] = res[:, r * LANES:(r + 1) * LANES]
                return carry

            lax.fori_loop(0, ROWS, wave, 0, unroll=4)

            def pack(n, carry):
                for u in range(8):
                    for r in range(2):
                        block = lstage[r, pl.ds((n * 8 + u) * PITCH, ROWS), :].astype(jnp.bfloat16)
                        gs[n * 8 + u, pl.ds((gi * 2 + r) * ROWS, ROWS), lanes] = block
                return carry

            lax.fori_loop(0, latitudes // 8, pack, 0)

        def own(t, carry):
            gr[t, pl.ds(pl.multiple_of(d * rows, ROWS), rows), lanes] = gs[d * t_loc + t, :, lanes]
            return carry

        lax.fori_loop(0, t_loc, own, 0)

    x_copies, y_copies, kept = {}, [], []

    def send_lat(h):
        for g in range(t_groups):
            n, lanes = h * t_groups + g, pl.ds(h * LANES, LANES)
            sent = []
            for e in lat_order(lat_count):
                dd = lax.rem(d + e, lat_count)
                sent.append(pltpu.make_async_remote_copy(
                    src_ref=gs.at[pl.ds(dd * t_loc + g * T_ROWS, T_ROWS), :, lanes],
                    dst_ref=gr.at[pl.ds(g * T_ROWS, T_ROWS), pl.ds(pl.multiple_of(d * rows, ROWS), rows), lanes],
                    send_sem=x_send.at[n, e - 1], recv_sem=x_recv.at[n, e - 1],
                    device_id={'lat': dd}, device_id_type=MESH))
                sent[-1].start()
            x_copies[n] = sent

    def to_grid(h, g):
        n = h * t_groups + g
        for copy in x_copies[n]:
            copy.wait_recv()

        def transform(i, carry):
            spec = gr[g * T_ROWS + i, :, pl.ds(h * LANES, LANES)]
            wave = lax.dot_general(spec, dft_ref[...], tn, preferred_element_type=jnp.float32)
            for b in range(lon_count):
                ystage[b, pl.ds(i, LANES, stride=T_ROWS), :] = wave[:, b * LANES:(b + 1) * LANES]
            return carry

        lax.fori_loop(0, T_ROWS, transform, 0)
        for q in lon_order(lon_count) + [0]:
            kk = lax.rem(k + q, lon_count)

            def pack(r, carry, q=q, kk=kk):
                block = ystage[kk, pl.ds(pl.multiple_of(r * (8 * T_ROWS), T_ROWS), 8 * T_ROWS), :]
                block = block.reshape(8, T_ROWS, LANES).astype(jnp.bfloat16)
                ys[q, pl.ds(h * LANES + r * 8, 8), pl.ds(g * T_ROWS, T_ROWS), :] = block
                return carry

            lax.fori_loop(0, LANES // 8, pack, 0)
            part = (pl.ds(h * LANES, LANES), pl.ds(g * T_ROWS, T_ROWS))
            src, dst = ys.at[(q,) + part], out_ref.at[(k,) + part]
            if q == 0:
                copy = pltpu.make_async_copy(src, dst, keep_sem.at[n])
                kept.append(copy)
            else:
                copy = pltpu.make_async_remote_copy(
                    src_ref=src, dst_ref=dst, send_sem=y_send.at[n, q - 1], recv_sem=y_recv.at[n, q - 1],
                    device_id={'lon': kk}, device_id_type=MESH)
                y_copies.append(copy)
            copy.start()

    pending = []
    for h in range(halves):
        if h == 0:
            mix(h, 0, blocks)
            load_tables.wait()
        else:
            cuts = [0, blocks // 2, 3 * blocks // 4, blocks]
            for first, last in zip(cuts, cuts[1:]):
                mix(h, first, last)
                if pending:
                    to_grid(*pending.pop(0))
        legendre_back(h)
        send_lat(h)
        pending += [(h, g) for g in range(t_groups)]
    for chunk in pending:
        to_grid(*chunk)
    for sent in x_copies.values():
        for copy in sent:
            copy.wait_send()
    for copy in kept:
        copy.wait()
    for copy in y_copies:
        copy.wait_send()
        copy.wait_recv()


def legendre_kernel(transposed, base_ref, table_ref, in_ref, out_ref, stage):
    step = pl.program_id(1)
    dims = (((0,), (0,)), ((), ())) if transposed else (((1,), (0,)), ((), ()))
    size = out_ref.shape[0]
    halves = in_ref.shape[4] // LANES
    for w in range(WAVES):
        table = table_ref[w].astype(jnp.bfloat16)
        for r in range(2):
            res = lax.dot_general(table, in_ref[0, r, w], dims, preferred_element_type=jnp.float32)
            for h in range(halves):
                stage[r, h, pl.ds(step * WAVES + w, size, stride=PITCH), :] = res[:, h * LANES:(h + 1) * LANES]

    @pl.when(step == ROWS // WAVES - 1)
    def _():
        def pack(n, carry):
            for r in range(2):
                for h in range(halves):
                    for u in range(8):
                        block = stage[r, h, pl.ds((n * 8 + u) * PITCH, ROWS), :].astype(jnp.bfloat16)
                        out_ref[n * 8 + u, pl.ds(r * ROWS, ROWS), pl.ds(h * LANES, LANES)] = block
            return carry

        lax.fori_loop(0, size // 8, pack, 0)


def legendre(table, values, base, transposed):
    groups, _, _, length, channels = values.shape
    size = table.shape[2] if transposed else table.shape[1]
    return pl.pallas_call(
        functools.partial(legendre_kernel, transposed),
        out_shape=jax.ShapeDtypeStruct((size, groups * 2 * ROWS, channels), jnp.bfloat16),
        grid_spec=pltpu.PrefetchScalarGridSpec(
            num_scalar_prefetch=1, grid=(groups, ROWS // WAVES),
            in_specs=[
                pl.BlockSpec((WAVES,) + table.shape[1:], lambda g, i, base_ref: (base_ref[0] + g * (ROWS // WAVES) + i, 0, 0)),
                pl.BlockSpec((1, 2, WAVES, length, channels), lambda g, i, base_ref: (g, 0, i, 0, 0)),
            ],
            out_specs=pl.BlockSpec((size, 2 * ROWS, channels), lambda g, i, base_ref: (0, g, 0)),
            scratch_shapes=[pltpu.VMEM((2, channels // LANES, size * PITCH, LANES), jnp.float32)]),
        compiler_params=pltpu.CompilerParams(vmem_limit_bytes=VMEM_LIMIT),
        name='legendre_back' if transposed else 'legendre_fwd',
    )(base, table, values)


def solution(mesh):
    lon_count, lat_count = mesh.shape['lon'], mesh.shape['lat']
    grid_spec = P('member', None, 'lat', 'lon')
    any_spec = pl.BlockSpec(memory_space=pl.ANY)
    vmem_spec = pl.BlockSpec(memory_space=pltpu.VMEM)
    dma = pltpu.SemaphoreType.DMA

    def local_layer(field_in, fwd_table, inv_table, mix_weights):
        samples, channels, t_loc, j_loc = field_in.shape
        degrees, latitudes = fwd_table.shape[1], fwd_table.shape[2]
        lon_points = j_loc * lon_count
        m_loc = degrees // lat_count
        groups, rows = m_loc // ROWS, 2 * m_loc
        n_chunks = (channels // LANES) * (t_loc // T_ROWS)
        fwd_dft, inv_dft = dft_tables(lon_points, degrees, lat_count)
        base = (lax.axis_index('lat') * (m_loc // WAVES)).astype(jnp.int32).reshape(1)

        spec = pl.pallas_call(
            functools.partial(to_spectral_kernel, lon_count, lat_count, t_loc),
            out_shape=jax.ShapeDtypeStruct((rows, latitudes, channels), jnp.bfloat16),
            in_specs=[any_spec, vmem_spec],
            out_specs=any_spec,
            scratch_shapes=[
                pltpu.VMEM((samples, channels * t_loc, j_loc), jnp.float32),
                pltpu.VMEM((samples - 1, t_loc, channels, j_loc), jnp.bfloat16),
                pltpu.VMEM((lon_count, t_loc, channels, j_loc), jnp.bfloat16),
                pltpu.VMEM((lat_count * rows * T_ROWS, LANES), jnp.float32),
                pltpu.VMEM((lat_count, rows, t_loc, channels), jnp.bfloat16),
                dma((channels // LANES, samples)),
                dma((n_chunks, lon_count - 1)), dma((n_chunks, lon_count - 1)),
                dma((n_chunks, lat_count - 1)), dma((n_chunks, lat_count - 1)),
                dma((n_chunks,)),
            ],
            compiler_params=pltpu.CompilerParams(collective_id=0, has_side_effects=True, vmem_limit_bytes=VMEM_LIMIT),
            name='to_spectral',
        )(field_in.reshape(samples, channels * t_loc, j_loc), fwd_dft)

        coef = legendre(fwd_table, spec.reshape(groups, 2, ROWS, latitudes, channels), base, False)
        tiles = channels // LANES
        w_rows = mix_weights.reshape(degrees, channels, tiles, LANES, 2)
        w_rows = jnp.transpose(w_rows, (0, 1, 2, 4, 3)).reshape(degrees, channels * 2 * tiles, LANES)
        wave = pl.pallas_call(
            functools.partial(mix_to_grid_kernel, lon_count, lat_count, t_loc),
            out_shape=jax.ShapeDtypeStruct((samples, channels, t_loc, j_loc), jnp.bfloat16),
            in_specs=[any_spec, any_spec, any_spec, vmem_spec],
            out_specs=any_spec,
            scratch_shapes=[
                pltpu.VMEM((2, ROWS, LANES * 2 * tiles, LANES), jnp.float32),
                pltpu.VMEM((2, ROWS, rows, channels), jnp.bfloat16),
                pltpu.VMEM((rows, degrees, LANES), jnp.bfloat16),
                pltpu.VMEM((rows * PITCH, LANES), jnp.float32),
                pltpu.VMEM((m_loc, degrees, latitudes), jnp.float32),
                pltpu.VMEM((2, latitudes * PITCH, LANES), jnp.float32),
                pltpu.VMEM((latitudes, rows, channels), jnp.bfloat16),
                pltpu.VMEM((t_loc, lat_count * rows, channels), jnp.bfloat16),
                pltpu.VMEM((lon_count, LANES * T_ROWS, LANES), jnp.float32),
                pltpu.VMEM((lon_count, channels, t_loc, j_loc), jnp.bfloat16),
                dma((2,)), dma((2,)), dma,
                dma((n_chunks, lat_count - 1)), dma((n_chunks, lat_count - 1)),
                dma((n_chunks, lon_count - 1)), dma((n_chunks, lon_count - 1)),
                dma((n_chunks,)),
            ],
            compiler_params=pltpu.CompilerParams(collective_id=1, has_side_effects=True, vmem_limit_bytes=VMEM_LIMIT),
            name='mix_to_grid',
        )(coef, w_rows, inv_table, inv_dft)
        return field_in + jax.nn.gelu(wave.astype(jnp.float32), approximate=True)

    whole = P(None, None, None)
    return jax.shard_map(local_layer, mesh=mesh, in_specs=(grid_spec, whole, whole, P(None, None, None, None)),
                         out_specs=grid_spec, check_vma=False)
```

time: 402 us -> 305 us (0.76)
  Pallas kernels: 379 us -> 284 us
    pallas_call x2 -> x1, Pallas kernels: 58.7 us -> 13.8 us  [legendre(): pl.pallas_call(functools.partial(legendre_kernel, transposed), out_shape=...]
    pallas_call x2 -> x1, Pallas kernels: 187 us -> 147 us  [local_layer(): pl.pallas_call(functools.partial(mix_to_grid_kernel, lon_count, lat_count...]
    pallas_call x1, Pallas kernels: 133 us -> 123 us  [local_layer(): pl.pallas_call(functools.partial(to_spectral_kernel, lon_count, lat_count...]
where the time goes in v2:
time: 305 us
  Pallas kernels  284 us (93%)
  other arithmetic  21.2 us (7%)
    pallas_call x1, Pallas kernels, local_layer(): pl.pallas_call(functools.partial(mix_to_grid_kernel, lon_count, lat_count...  147 us
    pallas_call x1, Pallas kernels, local_layer(): pl.pallas_call(functools.partial(to_spectral_kernel, lon_count, lat_count...  123 us
    add x1, other arithmetic, local_layer(): return field_in + jax.nn.gelu(wave.astype(jnp.float32), approximate=True)  15.4 us
    pallas_call x1, Pallas kernels, legendre(): pl.pallas_call(functools.partial(legendre_kernel, transposed), out_shape=...  13.8 us

profile of v2, /device:TPU:97, one launch (start us, length us, event | category | flops | bytes accessed | tf_op | source)
XLA Modules:
  0.0 305.2 jit_solution(12856580676075350798)
XLA Ops:
  0.0 0.1 mul.64
  0.1 0.1 eq.32
  0.2 5.8 %multiply_convert_fusion = (bf16[512,512]{1,0:T(8,128)(2,1)}, bf16[512,512]{1,0:T(8,128)(2,1)}) fusion(f32[512]{0:T(512)S(1)} %compare_select_fusion, s32[512]{0:T(512)S(1)} %mul.64, pred[512]{0:T(512)(128)(4,1)S(1)} %eq.32), kind=kLoop, calls=%fused_computation.16 | loop fusion | flops 4980736 | bytes 1053184 | tf_op jit(solution)/shard_map/convert_element_type | solution.py:34
  6.0 123.4 %to_spectral.1 = bf16[64,256,256]{2,1,0:T(8,128)(2,1)} custom-call(f32[4,8192,128]{2,1,0:T(8,128)} %bitcast.8, bf16[512,512]{1,0:T(8,128)(2,1)} %get-tuple-element.6.dft_ref), custom_call_target="tpu_custom_call" | custom-call | tf_op jit(solution)/shard_map/to_spectral/pallas_call | solution.py:376
  129.4 13.8 %legendre_fwd.1.coef_ref = bf16[256,64,256]{2,1,0:T(8,128)(2,1)} custom-call(s32[1]{0:T(128)} %bitcast.base_ref, f32[256,256,256]{2,1,0:T(8,128)} %table_ref.2, bf16[2,2,16,256,256]{4,3,2,1,0:T(8,128)(2,1)} %bitcast.9), custom_call_target="tpu_custom_call" | custom-call | tf_op jit(solution)/shard_map/legendre_fwd/pallas_call | solution.py:343
  143.2 146.6 %mix_to_grid.1 = bf16[4,256,32,128]{3,2,1,0:T(8,128)(2,1)} custom-call(bf16[256,64,256]{2,1,0:T(8,128)(2,1)} %legendre_fwd.1.coef_ref, f32[256,1024,128]{2,1,0:T(8,128)} %bitcast.5.w_ref, f32[256,256,256]{2,1,0:T(8,128)} %table_ref.3, bf16[512,512]{1,0:T(8,128)(2,1)} %get-tuple-element.5.dft_ref), custom_call_target="tpu_custom_call" | custom-call | tf_op jit(solution)/shard_map/mix_to_grid/pallas_call | solution.py:400
  289.8 15.4 %fusion.5 = f32[4,256,32,128]{3,2,1,0:T(8,128)} fusion(f32[4,256,32,128]{3,2,1,0:T(8,128)} %param.4, bf16[4,256,32,128]{3,2,1,0:T(8,128)(2,1)} %mix_to_grid.1), kind=kLoop, calls=%fused_computation.9 | loop fusion | flops 41943040 | bytes 41943040 | tf_op jit(solution)/shard_map/add | solution.py:424
  (4 shorter events, 0.0 us)
